TPU v7x, 32 devices: a whole 2x2x4 slice. The times are simulated.
32 devices in a mesh: seq: 2 (over core), batch: 16 (over z, y, x).
Axes of the slice: x: 2, y: 2, z: 4, core: 2. Of those that a mesh axis runs over, the one named last changes fastest.
Arguments:
- queries: bfloat16 [16, 1024, 1024], P('batch', 'seq'), may hold values from -6 to 6
- keys: bfloat16 [16, 1024, 1024], P('batch', 'seq'), may hold values from -6 to 6
- values: bfloat16 [16, 1024, 2048], P('batch', 'seq'), may hold values from -6 to 6
- gate_rate: bfloat16 [16, 1024, 1024], P('batch', 'seq'), may hold values from 0.5 to 2
- segment_ids: int32 [16, 1024], P('batch', 'seq'), may hold values from 0 to 2, never falling along the last dimension, each value on 1 to 512 neighbouring positions
- decay_exps: int32 [4], replicated, may hold values from 0 to 13
- out_weight: bfloat16 [2048, 2048], P('batch'), may hold values from -0.125 to 0.125
Outputs:
- projected: bfloat16 [16, 1024, 2048], P('batch', 'seq')
Inputs may be any that keep to these rules, and one draw needn't show every extreme that they name: `segment_ids`: within each stream the ids never fall and start at 0; each of the 3 ids covers 1 to 512 consecutive tokens, one of them exactly 512.
All inputs are finite; a program needn't handle non-finite values.
Results may differ from a plain program's by a relative error of at most 0.004.
The roundings to bfloat16 on the way count: a program that leaves them out, or rounds other values in their place, can miss the bound.
Values may be sent and summed in bfloat16 or wider, within the bound.
A program may use at most 128 MiB of HBM per device.

v0:
```python
import math

import jax
import jax.numpy as jnp
from jax import lax
from jax.sharding import PartitionSpec as P

BLOCK = 64


def shifted(block, axis, distance):
    devices = range(lax.axis_size(axis))
    route = [(i - distance, i) for i in devices if i - distance in devices]
    return lax.ppermute(block, axis, route)


def prefix(array, axis, combine, identity):
    peers, position = (lax.axis_size(axis), lax.axis_index(axis))
    everything = jax.tree.map(lambda part: lax.all_gather(part, axis), array)
    start = jax.tree.map(
        lambda part, zero: jnp.broadcast_to(jnp.asarray(zero, part.dtype), part.shape),
        array,
        identity,
    )

    def step(k, before):
        reached = k < position
        new = combine(before, jax.tree.map(lambda part: part[k], everything))
        return jax.tree.map(lambda a, b: jnp.where(reached, a, b), new, before)

    return lax.fori_loop(0, peers, step, start)


def linear_blocks(lifted_query, key_heads, value_heads, log_decay, starts, initial):
    groups, length, head_count, key_width = lifted_query.shape
    value_width = value_heads.shape[3]
    block_count = length // BLOCK

    def split(member):
        return jnp.swapaxes(member.reshape((groups, block_count, BLOCK) + member.shape[2:]), 0, 1)

    def advance(carried, pieces):
        query_rows, key_rows, value_rows, log_rows, start_rows = pieces
        running = jnp.cumsum(log_rows, axis=1)
        segment_rank = jnp.cumsum(start_rows, axis=1)
        unbroken = (segment_rank == 0).astype(jnp.float32)
        raised_q = query_rows * jnp.exp(running)
        raised_k = key_rows * jnp.exp(-running)
        scores = jnp.einsum("gthc,gshc->ghts", raised_q, raised_k, precision=lax.Precision.HIGHEST)
        order = jnp.arange(BLOCK)
        causal = order[:, None] >= order[None, :]
        same_doc = segment_rank[:, :, None] == segment_rank[:, None, :]
        allowed = jnp.logical_and(causal[None], same_doc).astype(jnp.float32)
        inside = jnp.einsum(
            "ghts,gshv->gthv",
            scores * allowed[:, None],
            value_rows,
            precision=lax.Precision.HIGHEST,
        )
        outside = unbroken[:, :, None, None] * jnp.einsum(
            "gthc,ghcv->gthv", raised_q, carried, precision=lax.Precision.HIGHEST
        )
        final_log = running[:, -1]
        in_last = (segment_rank == segment_rank[:, -1:]).astype(jnp.float32)
        weighted = key_rows * jnp.exp(final_log[:, None] - running) * in_last[:, :, None, None]
        kept = unbroken[:, -1][:, None, None, None] * jnp.exp(final_log)[..., None] * carried
        updated = kept + jnp.einsum(
            "gshc,gshv->ghcv", weighted, value_rows, precision=lax.Precision.HIGHEST
        )
        return (updated, inside + outside)

    members = (lifted_query, key_heads, value_heads, log_decay, starts)
    final, outputs = lax.scan(advance, initial, tuple((split(member) for member in members)))
    outputs = jnp.swapaxes(outputs, 0, 1).reshape(groups, length, head_count, value_width)
    return (outputs, final)


def combine(earlier, later):
    return (earlier[0] * later[0], later[0][..., None] * earlier[1] + later[1])


def local(queries, keys, values, gate_rate, segment_ids, decay_exps, out_weight):
    groups = queries.shape[0]
    length = queries.shape[1]
    head_count = decay_exps.shape[0]

    def heads_of(array):
        return array.astype(jnp.float32).reshape(groups, length, head_count, -1)

    scaling = jnp.exp2(-decay_exps.astype(jnp.float32)) / 16.0
    log_decay = -heads_of(gate_rate) * scaling[None, None, :, None]
    prior = shifted(segment_ids[:, -1:] + 1, "seq", 1) - 1
    previous = jnp.concatenate([prior, segment_ids[:, :-1]], axis=1)
    starts = (segment_ids != previous).astype(jnp.float32)
    key_heads = heads_of(keys)
    value_heads = heads_of(values)
    key_width = key_heads.shape[3]
    query_heads = heads_of(queries) * (1.0 / math.sqrt(key_width))
    initial = jnp.zeros((groups, head_count, key_width, value_heads.shape[3]), jnp.float32)
    local_out, local_state = linear_blocks(
        query_heads, key_heads, value_heads, log_decay, starts, initial
    )
    through = jnp.cumsum(log_decay, axis=1)
    unbroken = (jnp.cumsum(starts, axis=1) == 0).astype(jnp.float32)
    passing = unbroken[:, -1][:, None, None] * jnp.exp(through[:, -1])
    identity = (jnp.ones_like(passing), jnp.zeros_like(local_state))
    incoming = prefix((passing, local_state), "seq", combine, identity)[1]
    correction = unbroken[:, :, None, None] * jnp.einsum(
        "gthc,ghcv->gthv", query_heads * jnp.exp(through), incoming, precision=lax.Precision.HIGHEST
    )
    mixed = local_out + correction
    normed = mixed / jnp.sqrt(jnp.mean(mixed * mixed, axis=-1, keepdims=True) + 1.0)
    hidden = normed.astype(jnp.bfloat16).reshape(groups * length, -1)
    product = jnp.dot(
        hidden,
        lax.all_gather(out_weight, "batch", axis=0, tiled=True),
        preferred_element_type=jnp.float32,
    )
    return product.astype(jnp.bfloat16).reshape(groups, length, -1)


def solution(mesh):
    in_specs = (
        P("batch", "seq", None),
        P("batch", "seq", None),
        P("batch", "seq", None),
        P("batch", "seq", None),
        P("batch", "seq"),
        P(),
        P("batch", None),
    )
    out_specs = P("batch", "seq", None)
    return jax.shard_map(local, mesh=mesh, in_specs=in_specs, out_specs=out_specs, check_vma=False)
```

profile of v0, /device:TPU:0, one launch (start us, length us, event | category | flops | bytes accessed | tf_op | source)
XLA Modules:
  0.0 288.8 jit_solution(10949697371779731944)
XLA Ops:
  8.4 3.3 %collective-permute-start = (s32[1,1]{1,0:T(1,128)}, s32[1,1]{1,0:T(1,128)}, u32[]{:S(2)}, u32[]{:S(2)}) collective-permute-start(s32[1,1]{1,0:T(1,128)} %add.59), channel_id=1, source_target_pairs={{0,16},{1,17},{2,18},{3,19},{4,20},{5,21},{6,22},{7,23},{8,24},{9,... | collective-permute-start | bytes 20 | tf_op jit(solution)/shard_map/ppermute | solution.py:14
  16.4 1.6 convert_multiply_fusion
  18.1 2.9 copy.84
  20.9 3.2 %neg.34 = f32[8,1,64,4,256]{4,3,2,0,1:T(4,128)} reshape(f32[1,512,1024]{2,1,0:T(8,128)} %copy.84) | data formatting | bytes 4194304 | tf_op jit(solution)/shard_map/neg | solution.py:91
  24.1 4.4 %reshape.392 = f32[8,1,64,4,256]{2,0,4,3,1:T(8,128)} reshape(f32[1,512,1024]{1,2,0:T(8,128)} %convert_multiply_fusion) | data formatting | bytes 4194304 | tf_op jit(solution)/shard_map/mul | solution.py:98
  28.5 3.8 %copy.89 = f32[8,1,64,4,256]{4,3,2,1,0:T(4,128)} copy(f32[8,1,64,4,256]{2,0,4,3,1:T(8,128)} %reshape.392) | data formatting | bytes 4194304
  32.3 6.1 %reshape.386 = f32[8,1,64,4,512]{4,3,2,0,1:T(4,128)} reshape(bf16[1,512,2048]{2,1,0:T(8,128)(2,1)} %param.13) | data formatting | bytes 6291456 | tf_op jit(solution)/shard_map/transpose;reshape;reshape | solution.py:40
  38.4 1.9 reshape.385
  40.3 3.4 %multiply_bitcast_fusion.2 = f32[8,1,64,4,256]{4,3,2,1,0:T(4,128)} fusion(f32[8,1,64,4,256]{4,3,2,0,1:T(4,128)} %neg.34, f32[4]{0:T(128)S(1)} %exponential_multiply_fusion.1), kind=kLoop, calls=%fused_computation.60 | loop fusion | flops 524288 | bytes 4194320
  45.6 93.7 %while.27 = (s32[]{:T(128)}, f32[1,4,256,512]{3,2,1,0:T(8,128)S(1)}, f32[8,1,64,4,512]{4,2,0,3,1:T(8,128)}, f32[8,1,64]{2,1,0:T(1,128)S(1)}, f32[8,1,64,4,256]{4...) while((s32[]{:T(128)}, ...), condition=%wide.region_3.4_spmd.clone, body=%wide.region_0.3_spmd.clone.sunk | while | flops 963220736 | bytes 13299679 | solution.py:73
  55.0 2.3 bitcast_add_fusion.7
  66.7 2.3 bitcast_add_fusion.7
  78.4 2.3 bitcast_add_fusion.7
  90.2 2.3 bitcast_add_fusion.7
  101.9 2.3 bitcast_add_fusion.7
  113.6 2.3 bitcast_add_fusion.7
  125.3 2.3 bitcast_add_fusion.7
  137.0 2.3 bitcast_add_fusion.7
  141.4 3.3 %multiply_bitcast_fusion.1 = f32[1,256,4,512]{3,1,2,0:T(8,128)} fusion(f32[1,512,4,256]{1,3,2,0:T(8,128)} %bitcast.179, f32[4]{0:T(128)S(1)} %exponential_multiply_fusion.1), kind=kLoop, calls=%fused_computation.58 | loop fusion | flops 524288 | bytes 4194320 | tf_op jit(solution)/shard_map/transpose
  144.7 2.9 %copy.91 = f32[1,256,4,512]{1,3,2,0:T(8,128)} copy(f32[1,256,4,512]{3,1,2,0:T(8,128)} %multiply_bitcast_fusion.1) | data formatting | bytes 4194304 | tf_op jit(solution)/shard_map/transpose
  147.6 3.2 %fusion.35 = f32[1,256,4,4,128]{1,3,2,4,0:T(4,128)S(1)} fusion(f32[1,256,4,4,128]{1,4,3,2,0:T(8,128)} %bitcast.180), kind=kOutput, calls=%fused_computation.55 | output fusion | flops 66584576 | bytes 4194304 | tf_op jit(solution)/shard_map/reduce-window.2
  150.8 2.5 copy.93
  153.3 3.0 %copy.97 = f32[1,512,4,256]{3,2,1,0:T(4,128)} copy(f32[1,512,4,256]{1,3,2,0:T(8,128)} %bitcast.178) | data formatting | bytes 4194304 | tf_op jit(solution)/shard_map/mul | solution.py:98
  156.3 6.2 %multiply_bitcast_fusion = (f32[512,4,256]{2,1,0:T(4,128)}, f32[1,256,4,512]{1,2,3,0:T(4,128)}) fusion(f32[1,512,4,256]{3,2,1,0:T(4,128)} %copy.97, f32[256,4,4]{0,1,2:T(4,128)S(1)} %copy.94, f32[1,256,4,512]{1,3,2,0:T(8,128)} %bitcast.181), kind=kLoop, calls=%fused_computation.57 | loop fusion | flops 1048576 | bytes 8404992 | tf_op jit(solution)/shard_map/reshape.37
  165.8 5.4 %copy.100 = f32[1,512,4,512]{1,3,2,0:T(8,128)} copy(f32[1,512,4,512]{3,1,2,0:T(8,128)} %bitcast.182) | data formatting | bytes 8388608 | tf_op jit(solution)/shard_map/reshape;transpose | solution.py:74
  171.8 2.0 all_gather.13
  173.9 4.4 %while.28 = (s32[]{:T(128)}, f32[1,4,256,512]{3,2,1,0:T(8,128)S(1)}, s32[]{:T(128)}, f32[2,1,4,256]{3,2,1,0:T(4,128)S(1)}, f32[2,1,4,256,512]{4,3,2,1,0:T(8,128)}, /*index=5*/s32[]{:T(128)}, s32[]{:T(128)}) while((s32[]{:T(128)}, f32[1,4,256,512]{3,2,1,0:T(8,128)S(1)}, s32[]{:T(128)}, f32[2,1,4,256]{3,2,1,0:T(4,128)S(1)}, ...), condition=%wide.region_9.10_spmd.clone, body=%wide.region_8.9_spmd.clone.sunk | while | flops 2097156 | bytes 6303849 | solution.py:31
  173.9 2.2 fusion.71
  176.2 2.2 fusion.71
  178.4 9.6 %multiply_reduce_fusion = (f32[512,4]{0,1:T(4,128)S(1)}, f32[1,512,4,512]{1,3,2,0:T(8,128)S(1)}) fusion(f32[1,512,4,512]{1,3,2,0:T(8,128)} %copy.100, f32[512,4,256]{2,1,0:T(4,128)} %get-tuple-element.281, f32[1,4,256,512]{3,2,1,0:T(8,128)S(1)} %get-tuple-element.144, f32[512]{0:T(512)S(1)} %fusion.39), kind=kOutput, calls=%fused_computation.49 | convolution fusion | flops 3225417728 | bytes 12593152 | tf_op jit(solution)/shard_map/gthc,ghcv->gthv/dot_general | solution.py:108
  188.6 84.2 %all-gather.4.cloned.1.call-done = bf16[2048,2048]{1,0:T(8,128)(2,1)} async-done(((bf16[128,2048]{1,0:T(8,128)(2,1)}), bf16[2048,2048]{1,0:T(8,128)(2,1)}) %all-gather.4.cloned.1.call-update) | async-done | bytes 8388624 | tf_op jit(solution)/shard_map/all_gather | solution.py:116
  272.8 9.1 %fusion.32 = bf16[1,512,2048]{2,1,0:T(8,128)(2,1)} fusion(bf16[512,2048]{0,1:T(8,128)(2,1)S(1)} %bitcast.184, bf16[2048,2048]{1,0:T(8,128)(2,1)} %all-gather.4.cloned.1.call-done), kind=kOutput, calls=%fused_computation.51 | convolution fusion | flops 4296015872 | bytes 12582912 | tf_op jit(solution)/shard_map/dot_general | solution.py:114
  (162 shorter events, 83.0 us)
Async XLA Ops:
  6.5 167.4 %all-gather.6.cloned.1.call-start = ((), (), s32[]{:S(2)}) async-start(), calls=%async_computation.1 | async-start | bytes 6291456 | tf_op jit(solution)/shard_map/all_gather | solution.py:19
  8.4 35.3 %collective-permute-start = (s32[1,1]{1,0:T(1,128)}, s32[1,1]{1,0:T(1,128)}, u32[]{:S(2)}, u32[]{:S(2)}) collective-permute-start(s32[1,1]{1,0:T(1,128)} %add.59), channel_id=1, source_target_pairs={{0,16},{1,17},{2,18},{3,19},{4,20},{5,21},{6,22},{7,23},{8,24},{9,... | collective-permute-start | bytes 20 | tf_op jit(solution)/shard_map/ppermute | solution.py:14
  13.3 1.6 copy-start.3
  32.3 6.1 %copy-start.1 = (bf16[1,512,1024]{2,1,0:T(8,128)(2,1)S(1)}, bf16[1,512,1024]{2,1,0:T(8,128)(2,1)}, u32[]{:S(2)}) copy-start(bf16[1,512,1024]{2,1,0:T(8,128)(2,1)} %param.12) | copy-start | bytes 3145732
  40.3 4.6 %copy-start.2 = (s32[1,512]{1,0:T(1,128)S(1)}, s32[1,512]{1,0:T(1,128)}, u32[]{:S(2)}) copy-start(s32[1,512]{1,0:T(1,128)} %param.15) | copy-start | bytes 6148
  139.3 1.3 copy-start
  140.7 132.2 %all-gather.4.cloned.1.call-start = ((), (), s32[]{:S(2)}) async-start(), calls=%async_computation | async-start | bytes 8912896 | tf_op jit(solution)/shard_map/all_gather | solution.py:116
Sparse Core Ops, SparseCore 0:
  140.8 15.7 all-gather.5
  159.3 113.4 all-gather.3
where the time goes:
time: 291 us; the launch traced here: 289 us
  waiting for transfers between devices  84.8 us (29%)
  matrix products  64.5 us (22%)
  local copies, waits for them, and re-layouts  61.3 us (21%)
  other arithmetic  51.6 us (18%)
  between operations  16 us (5%)
  loops' own time  5.01 us (2%)
  starting transfers between devices  3.56 us (1%)
    all_gather x1, waiting for transfers between devices, local(): lax.all_gather(out_weight, 'batch', axis=0, tiled=True)  84.2 us
    dot_general x8, matrix products, advance(): jnp.einsum('gshc,gshv->ghcv', weighted, value_rows, precision=lax.Precisi...  18.2 us
    dot_general x8, matrix products, advance(): jnp.einsum('ghts,gshv->gthv', scores * allowed[:, None], value_rows, prec...  12.6 us
    dot_general x8, matrix products, advance(): jnp.einsum('gthc,ghcv->gthv', raised_q, carried, precision=lax.Precision....  11.5 us
    mul x8, other arithmetic, advance(): raised_k = key_rows * jnp.exp(-running)  10.1 us
    another operation x5, other arithmetic  9.91 us
    dot_general x1, matrix products, local(): jnp.einsum('gthc,ghcv->gthv', query_heads * jnp.exp(through), incoming, p...  9.6 us
    dot_general x1, matrix products, local(): jnp.dot(hidden, lax.all_gather(out_weight, 'batch', axis=0, tiled=True),...  9.1 us
  transfers between devices with their start and end apart: 3, of which 1 were waited for; matrix products, arithmetic and copies ran while one was open for 26% of the time, Pallas kernels for 0%

commit v1 on v0

v1 whole, which is shorter than its diff:
```python
import functools
import math

import jax
import jax.numpy as jnp
from jax import lax
from jax.experimental import pallas as pl
from jax.experimental.pallas import tpu as pltpu
from jax.sharding import PartitionSpec as P

MESH = pl.DeviceIdType.MESH
CHUNK = 256
TILE = 512


def chip_grid(mesh):
    count = mesh.shape["batch"]
    try:
        axis = mesh.axis_names.index("batch")
        line = mesh.devices.swapaxes(0, axis).reshape(count, -1)[:, 0]
        coords = [tuple(device.coords) for device in line]
        sizes = [len({c[i] for c in coords}) for i in (2, 1, 0)]
        lows = [min(c[i] for c in coords) for i in (2, 1, 0)]
        for index, c in enumerate(coords):
            z, y, x = (c[2] - lows[0], c[1] - lows[1], c[0] - lows[2])
            if (z * sizes[1] + y) * sizes[2] + x != index:
                return (count, 1, 1)
        return tuple(sizes)
    except Exception:
        return (count, 1, 1)


def split(x):
    high = x.astype(jnp.bfloat16)
    return high, (x - high.astype(jnp.float32)).astype(jnp.bfloat16)


def mm(a, b):
    return lax.dot_general(a, b, (((1,), (0,)), ((), ())), preferred_element_type=jnp.float32)


def mm_t(a, b):
    return lax.dot_general(a, b, (((1,), (1,)), ((), ())), preferred_element_type=jnp.float32)


def t_mm(a, b):
    return lax.dot_general(a, b, (((0,), (0,)), ((), ())), preferred_element_type=jnp.float32)


def kernel(
    grid, peers, heads, chunk,
    q_hbm, k_hbm, v_hbm, g_hbm, seg_ref, exps_ref, w_hbm,
    out_hbm,
    q_ref, k_ref, v_ref, g_ref, w_ref, hidden, acc, out_ref, seg_in, state_in, state_out,
    load_sem, out_sem, seg_sem, state_send, state_recv, send_sem, recv_sem, msend, mrecv,
):
    Z, Y, X = grid
    s = lax.axis_index("seq")
    me = lax.axis_index("batch")
    length, keys = q_ref.shape
    key_width = keys // heads
    value_width = v_ref.shape[1] // heads
    rows = w_hbm.shape[0]
    columns = w_ref.shape[1]
    part = columns // peers
    plane_rows = rows * X * Y
    a = me // (X * Y)
    swap = X == Y
    nb, nc = X, Y

    def strides(core):
        if not swap:
            return 1, X
        even = lax.rem(core, 2) == 0
        return jnp.where(even, 1, X), jnp.where(even, X, 1)

    def chip_back(core, da, db, dc):
        sb, sc = strides(core)
        b = lax.rem(me // sb, nb)
        c = lax.rem(me // sc, nc)
        return (
            lax.rem(a - da + Z, Z) * (X * Y)
            + lax.rem(b - db + nb, nb) * sb
            + lax.rem(c - dc + nc, nc) * sc
        )

    def label(da, db, dc):
        return (da * nb + db) * nc + dc

    def block(core, chip):
        return w_ref.at[
            pl.ds(pl.multiple_of(chip * rows, rows), rows),
            pl.ds(pl.multiple_of(core * part, part), part),
        ]

    def relay(held, step):
        da, db, dc = (h + t for h, t in zip(held, step))
        here = block(s, chip_back(s, *held))
        target = chip_back(s, -step[0], -step[1], -step[2])
        index = label(da, db, dc)
        return pltpu.make_async_remote_copy(
            src_ref=here, dst_ref=here, send_sem=send_sem.at[index], recv_sem=recv_sem.at[index],
            device_id={"batch": target}, device_id_type=MESH,
        )

    def arrival(da, db, dc):
        here = block(s, chip_back(s, da, db, dc))
        index = label(da, db, dc)
        other = lax.rem(me + 1, X * Y * Z)
        return pltpu.make_async_remote_copy(
            src_ref=here, dst_ref=here, send_sem=send_sem.at[index], recv_sem=recv_sem.at[index],
            device_id={"batch": other}, device_id_type=MESH,
        )

    def mirror(da, db, dc, ds, core):
        here = block(core, chip_back(core, da, db, dc))
        index = label(da, db, dc)
        return pltpu.make_async_remote_copy(
            src_ref=here, dst_ref=here,
            send_sem=msend.at[ds - 1, index], recv_sem=mrecv.at[ds - 1, index],
            device_id={"seq": lax.rem(s + ds, peers)}, device_id_type=MESH,
        )

    def share(da, db, dc):
        for ds in range(1, peers):
            mirror(da, db, dc, ds, s).start()

    def forward_plane(g):
        for db in range(1, nb):
            relay((g, 0, 0), (0, db, 0)).start()
        for dc in range(1, nc):
            relay((g, 0, 0), (0, 0, dc)).start()

    def middle(g):
        for db in range(1, nb):
            arrival(g, db, 0).wait_recv()
            for dc in range(1, nc):
                relay((g, db, 0), (0, 0, dc)).start()
            share(g, db, 0)

    def enter(g):
        @pl.when(g < Z)
        def _():
            arrival(g, 0, 0).wait_recv()
            forward_plane(g)
            share(g, 0, 0)

    def tail(g):
        for dc in range(1, nc):
            for db in range(nb):
                arrival(g, db, dc).wait_recv()
                share(g, db, dc)

    def mirrored(g):
        for ds in range(1, peers):
            core = lax.rem(s - ds + peers, peers)
            for db in range(nb):
                for dc in range(nc):
                    def wait():
                        mirror(g, db, dc, ds, core).wait_recv()
                    if db or dc:
                        wait()
                    else:
                        pl.when(g > 0)(wait)

    loads = [
        pltpu.make_async_copy(
            w_hbm, w_ref.at[pl.ds(pl.multiple_of(me * rows, rows), rows), :], load_sem.at[0]
        ),
        pltpu.make_async_copy(g_hbm, g_ref, load_sem.at[1]),
        pltpu.make_async_copy(k_hbm, k_ref, load_sem.at[2]),
        pltpu.make_async_copy(q_hbm, q_ref, load_sem.at[3]),
        pltpu.make_async_copy(v_hbm, v_ref, load_sem.at[4]),
    ]
    for load in loads:
        load.start()

    barrier = pltpu.get_barrier_semaphore()
    friends = [{"batch": chip_back(s, d, 0, 0)} for d in range(1, Z)]
    friends += [{"batch": chip_back(s, 0, d, 0)} for d in range(1, nb)]
    friends += [{"batch": chip_back(s, 0, 0, d)} for d in range(1, nc)]
    friends += [{"seq": lax.rem(s + d, peers)} for d in range(1, peers)]
    for friend in friends:
        pl.semaphore_signal(barrier, inc=1, device_id=friend, device_id_type=MESH)
    pl.semaphore_wait(barrier, len(friends))

    loads[0].wait()
    for da in range(1, Z):
        relay((0, 0, 0), (da, 0, 0)).start()
    forward_plane(0)

    def next_core():
        return {"seq": lax.rem(s + 1, peers)}

    seg_copy = pltpu.make_async_remote_copy(
        src_ref=seg_ref, dst_ref=seg_in, send_sem=seg_sem.at[0], recv_sem=seg_sem.at[1],
        device_id=next_core(), device_id_type=MESH,
    )

    def state_copy(h):
        return pltpu.make_async_remote_copy(
            src_ref=state_out.at[h], dst_ref=state_in.at[h],
            send_sem=state_send.at[h], recv_sem=state_recv.at[h],
            device_id=next_core(), device_id_type=MESH,
        )

    @pl.when(s < peers - 1)
    def _():
        seg_copy.start()

    @pl.when(s == 0)
    def _():
        state_in[...] = jnp.zeros_like(state_in)
        seg_in[...] = jnp.full(seg_in.shape, -1, jnp.int32)

    for load in loads[1:]:
        load.wait()

    @pl.when(s > 0)
    def _():
        seg_copy.wait_recv()

    order_t = lax.broadcasted_iota(jnp.int32, (chunk, chunk), 0)
    order_s = lax.broadcasted_iota(jnp.int32, (chunk, chunk), 1)
    causal = order_t >= order_s
    triangle = jnp.where(causal, 1.0, 0.0).astype(jnp.bfloat16)
    seg_row = seg_ref[...].astype(jnp.float32)
    before = seg_in[...].astype(jnp.float32)[:, length - 1:]
    seg_wide = jnp.broadcast_to(seg_row, (128, length)).T

    def head(h, _):
        exponent = jnp.full((1, key_width), exps_ref[h], jnp.int32).astype(jnp.float32)
        scale = jnp.exp2(-exponent) * (-1.0 / 16.0)

        @pl.when(s > 0)
        def _():
            state_copy(h).wait_recv()

        state = state_in[h]
        previous = before
        key_cols = pl.ds(pl.multiple_of(h * key_width, key_width), key_width)
        value_cols = pl.ds(pl.multiple_of(h * value_width, value_width), value_width)
        for i in range(length // chunk):
            now = pl.ds(i * chunk, chunk)
            log = mm(triangle, g_ref[now, key_cols]) * scale
            fall = jnp.exp(log)
            raised_q = q_ref[now, key_cols].astype(jnp.float32) * (fall * (1.0 / math.sqrt(key_width)))
            raised_k = k_ref[now, key_cols].astype(jnp.float32) * jnp.exp(-log)
            value = v_ref[now, value_cols]
            q_hi, q_lo = split(raised_q)
            k_hi, k_lo = split(raised_k)
            row = seg_row[:, i * chunk:(i + 1) * chunk]
            column = seg_wide[i * chunk:(i + 1) * chunk, :1]
            scores = mm_t(q_hi, k_hi) + mm_t(q_hi, k_lo) + mm_t(q_lo, k_hi)
            scores = jnp.where(jnp.logical_and(causal, column == row), scores, 0.0)
            p_hi, p_lo = split(scores)
            s_hi, s_lo = split(state)
            carried = mm_t(q_hi, s_hi) + mm_t(q_hi, s_lo) + mm_t(q_lo, s_hi)
            mixed = mm(p_hi, value) + mm(p_lo, value)
            mixed = mixed + jnp.where(column == previous, carried, 0.0)
            power = jnp.mean(mixed * mixed, axis=-1, keepdims=True)
            hidden[now, value_cols] = (mixed * lax.rsqrt(power + 1.0)).astype(jnp.bfloat16)
            final = fall[chunk - 1:, :]
            last = row[:, chunk - 1:]
            weighted = jnp.where(column == last, raised_k * final, 0.0)
            w_hi, w_lo = split(weighted)
            kept = jnp.where(last == previous, state * final, 0.0)
            state = kept + t_mm(value, w_hi) + t_mm(value, w_lo)
            previous = last

        @pl.when(s < peers - 1)
        def _():
            state_out[h] = state
            state_copy(h).start()

        @pl.when(h == (heads - 1) // 2)
        def _():
            middle(0)
            enter(1)

        return 0

    lax.fori_loop(0, heads, head, 0)

    def plane_start(g):
        return pl.multiple_of(lax.rem(a - g + Z, Z) * plane_rows, plane_rows)

    def project(g):
        start = plane_start(g)
        left = hidden[:, pl.ds(start, plane_rows)]
        for tile in range(columns // TILE):
            cols = pl.ds(tile * TILE, TILE)
            product = mm(left, w_ref[pl.ds(start, plane_rows), cols])

            @pl.when(g == 0)
            def _():
                acc[:, cols] = product

            @pl.when(g > 0)
            def _():
                acc[:, cols] += product

    def step(g, _):
        middle(g)
        enter(g + 1)
        tail(g - 1)
        mirrored(g - 1)
        project(g - 1)
        return 0

    lax.fori_loop(1, Z, step, 0)
    tail(Z - 1)
    mirrored(Z - 1)
    start = plane_start(Z - 1)
    left = hidden[:, pl.ds(start, plane_rows)]
    stores = []
    for tile in range(columns // TILE):
        cols = pl.ds(tile * TILE, TILE)
        product = mm(left, w_ref[pl.ds(start, plane_rows), cols])
        total = acc[:, cols] + product if Z > 1 else product
        out_ref[:, cols] = total.astype(jnp.bfloat16)
        store = pltpu.make_async_copy(out_ref.at[:, cols], out_hbm.at[:, cols], out_sem.at[tile])
        store.start()
        stores.append(store)

    @pl.when(s < peers - 1)
    def _():
        seg_copy.wait_send()

        def sent(h, _):
            state_copy(h).wait_send()
            return 0

        lax.fori_loop(0, heads, sent, 0)

    def sent_block(index, _):
        da, rest = index // (nb * nc), lax.rem(index, nb * nc)
        db, dc = rest // nc, lax.rem(rest, nc)
        arrival(da, db, dc).wait_send()
        for ds in range(1, peers):
            mirror(da, db, dc, ds, s).wait_send()
        return 0

    lax.fori_loop(1, Z * nb * nc, sent_block, 0)
    for store in stores:
        store.wait()


def local(grid, peers, queries, keys, values, gate_rate, segment_ids, decay_exps, out_weight):
    groups, length, key_features = queries.shape
    heads = decay_exps.shape[0]
    features = values.shape[2]
    columns = out_weight.shape[1]
    chips = grid[0] * grid[1] * grid[2]
    chunk = min(CHUNK, length)
    kw, vw = key_features // heads, features // heads
    bf16, f32 = jnp.bfloat16, jnp.float32
    anywhere = pl.BlockSpec(memory_space=pl.ANY)
    call = pl.pallas_call(
        functools.partial(kernel, grid, peers, heads, chunk),
        out_shape=jax.ShapeDtypeStruct((length, columns), bf16),
        in_specs=[anywhere] * 4
        + [pl.BlockSpec(memory_space=pltpu.VMEM), pl.BlockSpec(memory_space=pltpu.SMEM), anywhere],
        out_specs=anywhere,
        scratch_shapes=[
            pltpu.VMEM((length, key_features), bf16),
            pltpu.VMEM((length, key_features), bf16),
            pltpu.VMEM((length, features), bf16),
            pltpu.VMEM((length, key_features), bf16),
            pltpu.VMEM((features, columns), bf16),
            pltpu.VMEM((length, features), bf16),
            pltpu.VMEM((length, columns), f32),
            pltpu.VMEM((length, columns), bf16),
            pltpu.VMEM((1, length), jnp.int32),
            pltpu.VMEM((heads, vw, kw), f32),
            pltpu.VMEM((heads, vw, kw), f32),
            pltpu.SemaphoreType.DMA((5,)),
            pltpu.SemaphoreType.DMA((columns // TILE,)),
            pltpu.SemaphoreType.DMA((2,)),
            pltpu.SemaphoreType.DMA((heads,)),
            pltpu.SemaphoreType.DMA((heads,)),
            pltpu.SemaphoreType.DMA((chips,)),
            pltpu.SemaphoreType.DMA((chips,)),
            pltpu.SemaphoreType.DMA((max(peers - 1, 1), chips)),
            pltpu.SemaphoreType.DMA((max(peers - 1, 1), chips)),
        ],
        compiler_params=pltpu.CompilerParams(
            collective_id=0, has_side_effects=True, vmem_limit_bytes=60 * 1024 * 1024
        ),
        name="gla_project",
    )
    outs = [
        call(queries[n], keys[n], values[n], gate_rate[n], segment_ids[n:n + 1], decay_exps, out_weight)
        for n in range(groups)
    ]
    return jnp.stack(outs)


def solution(mesh):
    in_specs = (
        P("batch", "seq", None),
        P("batch", "seq", None),
        P("batch", "seq", None),
        P("batch", "seq", None),
        P("batch", "seq"),
        P(),
        P("batch", None),
    )
    body = functools.partial(local, chip_grid(mesh), mesh.shape["seq"])
    return jax.shard_map(
        body, mesh=mesh, in_specs=in_specs, out_specs=P("batch", "seq", None), check_vma=False
    )
```

time: 291 us -> 58.8 us (0.20)
  the two profiles are of different devices: /device:TPU:0 before, /device:TPU:17 now
where the time goes in v1:
time: 58.8 us; the launch traced here: 58.6 us
  Pallas kernels  55.4 us (94%)
  local copies, waits for them, and re-layouts  3.16 us (5%)
    pallas_call x1, Pallas kernels, local(): call(queries[n], keys[n], values[n], gate_rate[n], segment_ids[n:n + 1],...  55.4 us
    unnamed x1, local copies, waits for them, and re-layouts  3.16 us

profile of v1, /device:TPU:17, one launch (start us, length us, event | category | flops | bytes accessed | tf_op | source)
XLA Modules:
  0.0 58.6 jit_solution(14719599149838184326)
XLA Ops:
  0.0 55.4 %gla_project.1 = bf16[512,2048]{1,0:T(8,128)(2,1)} custom-call(bf16[512,1024]{1,0:T(8,128)(2,1)} %bitcast.7, bf16[512,1024]{1,0:T(8,128)(2,1)} %bitcast.8, bf16[512,2048]{1,0:T(8,128)(2,1)} %bitcast.6, bf16[512,1024]{1,0:T(8,128)(2,1)} %bitcast.9, s32[1,512]{1,0:T(1,128)} %seg_ref.1, s32[4]{0:T(128)} %exps_ref.1, bf16[128,2048]{1,0:T(8,128)(2,1)} %w_hbm.1), custom_call_target="tpu_custom_call" | custom-call | tf_op jit(solution)/shard_map/gla_project/pallas_call | solution.py:393
  55.4 3.2 %copy.9 = bf16[1,512,2048]{2,1,0:T(8,128)(2,1)} copy(bf16[1,512,2048]{2,1,0:T(8,128)(2,1)} %bitcast.5) | data formatting | bytes 4194304

commit v2 on v1

--- a/solution.py
+++ b/solution.py
@@ -50,9 +50,9 @@
 def kernel(
     grid, peers, heads, chunk,
     q_hbm, k_hbm, v_hbm, g_hbm, seg_ref, exps_ref, w_hbm,
-    out_hbm,
-    q_ref, k_ref, v_ref, g_ref, w_ref, hidden, acc, out_ref, seg_in, state_in, state_out,
-    load_sem, out_sem, seg_sem, state_send, state_recv, send_sem, recv_sem, msend, mrecv,
+    out_ref,
+    q_ref, k_ref, v_ref, g_ref, w_ref, hidden, acc, seg_in, state_in, state_out,
+    load_sem, seg_sem, state_send, state_recv, send_sem, recv_sem, climb_sem, msend, mrecv,
 ):
     Z, Y, X = grid
     s = lax.axis_index("seq")
@@ -74,18 +74,25 @@
         even = lax.rem(core, 2) == 0
         return jnp.where(even, 1, X), jnp.where(even, X, 1)
 
-    def chip_back(core, da, db, dc):
+    def chip_at(core, plane, db, dc):
         sb, sc = strides(core)
         b = lax.rem(me // sb, nb)
         c = lax.rem(me // sc, nc)
         return (
-            lax.rem(a - da + Z, Z) * (X * Y)
+            plane * (X * Y)
             + lax.rem(b - db + nb, nb) * sb
             + lax.rem(c - dc + nc, nc) * sc
         )
 
-    def label(da, db, dc):
-        return (da * nb + db) * nc + dc
+    near = jnp.minimum(a, Z - 1 - a)
+
+    def plane_at(g):
+        side = jnp.where(lax.rem(g, 2) == 1, -1, 1)
+        rest = jnp.where(a < Z - 1 - a, g, Z - 1 - g)
+        return jnp.where(g <= 2 * near, a + (g + 1) // 2 * side, rest)
+
+    def label(plane, db, dc):
+        return (plane * nb + db) * nc + dc
 
     def block(core, chip):
         return w_ref.at[
@@ -94,70 +101,95 @@
         ]
 
     def relay(held, step):
-        da, db, dc = (h + t for h, t in zip(held, step))
-        here = block(s, chip_back(s, *held))
-        target = chip_back(s, -step[0], -step[1], -step[2])
-        index = label(da, db, dc)
+        here = block(s, chip_at(s, *held))
+        target = chip_at(s, a, -step[0], -step[1])
+        index = label(held[0], held[1] + step[0], held[2] + step[1])
         return pltpu.make_async_remote_copy(
             src_ref=here, dst_ref=here, send_sem=send_sem.at[index], recv_sem=recv_sem.at[index],
             device_id={"batch": target}, device_id_type=MESH,
         )
 
-    def arrival(da, db, dc):
-        here = block(s, chip_back(s, da, db, dc))
-        index = label(da, db, dc)
+    def climb(plane, way):
+        here = block(s, chip_at(s, plane, 0, 0))
+        target = me + (X * Y if way else -X * Y)
+        return pltpu.make_async_remote_copy(
+            src_ref=here, dst_ref=here, send_sem=climb_sem.at[way, plane],
+            recv_sem=recv_sem.at[label(plane, 0, 0)],
+            device_id={"batch": target}, device_id_type=MESH,
+        )
+
+    def arrival(plane, db, dc):
+        here = block(s, chip_at(s, plane, db, dc))
+        index = label(plane, db, dc)
         other = lax.rem(me + 1, X * Y * Z)
         return pltpu.make_async_remote_copy(
             src_ref=here, dst_ref=here, send_sem=send_sem.at[index], recv_sem=recv_sem.at[index],
             device_id={"batch": other}, device_id_type=MESH,
         )
 
-    def mirror(da, db, dc, ds, core):
-        here = block(core, chip_back(core, da, db, dc))
-        index = label(da, db, dc)
+    def mirror(plane, db, dc, ds, core):
+        here = block(core, chip_at(core, plane, db, dc))
+        index = label(plane, db, dc)
         return pltpu.make_async_remote_copy(
             src_ref=here, dst_ref=here,
             send_sem=msend.at[ds - 1, index], recv_sem=mrecv.at[ds - 1, index],
             device_id={"seq": lax.rem(s + ds, peers)}, device_id_type=MESH,
         )
 
-    def share(da, db, dc):
+    def share(plane, db, dc):
         for ds in range(1, peers):
-            mirror(da, db, dc, ds, s).start()
-
-    def forward_plane(g):
+            mirror(plane, db, dc, ds, s).start()
+
+    def forward_plane(plane):
         for db in range(1, nb):
-            relay((g, 0, 0), (0, db, 0)).start()
+            relay((plane, 0, 0), (db, 0)).start()
         for dc in range(1, nc):
-            relay((g, 0, 0), (0, 0, dc)).start()
+            relay((plane, 0, 0), (0, dc)).start()
 
     def middle(g):
-        for db in range(1, nb):
-            arrival(g, db, 0).wait_recv()
-            for dc in range(1, nc):
-                relay((g, db, 0), (0, 0, dc)).start()
-            share(g, db, 0)
+        @pl.when(g < Z)
+        def _():
+            plane = plane_at(g)
+            for db in range(1, nb):
+                arrival(plane, db, 0).wait_recv()
+                for dc in range(1, nc):
+                    relay((plane, db, 0), (0, dc)).start()
+                share(plane, db, 0)
 
     def enter(g):
         @pl.when(g < Z)
         def _():
-            arrival(g, 0, 0).wait_recv()
-            forward_plane(g)
-            share(g, 0, 0)
+            plane = plane_at(g)
+            arrival(plane, 0, 0).wait_recv()
+
+            @pl.when(jnp.logical_and(plane < a, a < Z - 1))
+            def _():
+                climb(plane, 1).start()
+
+            @pl.when(jnp.logical_and(plane > a, a > 0))
+            def _():
+                climb(plane, 0).start()
+
+            forward_plane(plane)
+            share(plane, 0, 0)
 
     def tail(g):
-        for dc in range(1, nc):
-            for db in range(nb):
-                arrival(g, db, dc).wait_recv()
-                share(g, db, dc)
+        @pl.when(g < Z)
+        def _():
+            plane = plane_at(g)
+            for dc in range(1, nc):
+                for db in range(nb):
+                    arrival(plane, db, dc).wait_recv()
+                    share(plane, db, dc)
 
     def mirrored(g):
+        plane = plane_at(g)
         for ds in range(1, peers):
             core = lax.rem(s - ds + peers, peers)
             for db in range(nb):
                 for dc in range(nc):
                     def wait():
-                        mirror(g, db, dc, ds, core).wait_recv()
+                        mirror(plane, db, dc, ds, core).wait_recv()
                     if db or dc:
                         wait()
                     else:
@@ -176,18 +208,34 @@
         load.start()
 
     barrier = pltpu.get_barrier_semaphore()
-    friends = [{"batch": chip_back(s, d, 0, 0)} for d in range(1, Z)]
-    friends += [{"batch": chip_back(s, 0, d, 0)} for d in range(1, nb)]
-    friends += [{"batch": chip_back(s, 0, 0, d)} for d in range(1, nc)]
+    friends = [{"batch": chip_at(s, a, d, 0)} for d in range(1, nb)]
+    friends += [{"batch": chip_at(s, a, 0, d)} for d in range(1, nc)]
     friends += [{"seq": lax.rem(s + d, peers)} for d in range(1, peers)]
     for friend in friends:
         pl.semaphore_signal(barrier, inc=1, device_id=friend, device_id_type=MESH)
-    pl.semaphore_wait(barrier, len(friends))
+
+    @pl.when(a < Z - 1)
+    def _():
+        pl.semaphore_signal(barrier, inc=1, device_id={"batch": me + X * Y}, device_id_type=MESH)
+
+    @pl.when(a > 0)
+    def _():
+        pl.semaphore_signal(barrier, inc=1, device_id={"batch": me - X * Y}, device_id_type=MESH)
+
+    above, below = jnp.where(a < Z - 1, 1, 0), jnp.where(a > 0, 1, 0)
+    pl.semaphore_wait(barrier, len(friends) + above + below)
 
     loads[0].wait()
-    for da in range(1, Z):
-        relay((0, 0, 0), (da, 0, 0)).start()
-    forward_plane(0)
+
+    @pl.when(a < Z - 1)
+    def _():
+        climb(a, 1).start()
+
+    @pl.when(a > 0)
+    def _():
+        climb(a, 0).start()
+
+    forward_plane(a)
 
     def next_core():
         return {"seq": lax.rem(s + 1, peers)}
@@ -228,7 +276,26 @@
     before = seg_in[...].astype(jnp.float32)[:, length - 1:]
     seg_wide = jnp.broadcast_to(seg_row, (128, length)).T
 
+    def first():
+        middle(0)
+        enter(1)
+
+    def second():
+        enter(2)
+        middle(1)
+
+    def third():
+        enter(3)
+        tail(0)
+
+    events = [first, second, third]
+    early = min(len(events), heads - 1)
+
     def head(h, _):
+        turn = h - jnp.where(s == 0, 1, 0)
+        for number, event in enumerate(events[:early]):
+            pl.when(turn == number)(event)
+
         exponent = jnp.full((1, key_width), exps_ref[h], jnp.int32).astype(jnp.float32)
         scale = jnp.exp2(-exponent) * (-1.0 / 16.0)
 
@@ -273,17 +340,14 @@
             state_out[h] = state
             state_copy(h).start()
 
-        @pl.when(h == (heads - 1) // 2)
-        def _():
-            middle(0)
-            enter(1)
-
         return 0
 
     lax.fori_loop(0, heads, head, 0)
+    for event in events[early:]:
+        event()
 
     def plane_start(g):
-        return pl.multiple_of(lax.rem(a - g + Z, Z) * plane_rows, plane_rows)
+        return pl.multiple_of(plane_at(g) * plane_rows, plane_rows)
 
     def project(g):
         start = plane_start(g)
@@ -301,27 +365,22 @@
                 acc[:, cols] += product
 
     def step(g, _):
-        middle(g)
-        enter(g + 1)
-        tail(g - 1)
-        mirrored(g - 1)
-        project(g - 1)
+        middle(g + 2)
+        enter(g + 4)
+        mirrored(g)
+        project(g)
+        tail(g + 1)
         return 0
 
-    lax.fori_loop(1, Z, step, 0)
-    tail(Z - 1)
+    lax.fori_loop(0, Z - 1, step, 0)
     mirrored(Z - 1)
     start = plane_start(Z - 1)
     left = hidden[:, pl.ds(start, plane_rows)]
-    stores = []
     for tile in range(columns // TILE):
         cols = pl.ds(tile * TILE, TILE)
         product = mm(left, w_ref[pl.ds(start, plane_rows), cols])
         total = acc[:, cols] + product if Z > 1 else product
         out_ref[:, cols] = total.astype(jnp.bfloat16)
-        store = pltpu.make_async_copy(out_ref.at[:, cols], out_hbm.at[:, cols], out_sem.at[tile])
-        store.start()
-        stores.append(store)
 
     @pl.when(s < peers - 1)
     def _():
@@ -333,17 +392,32 @@
 
         lax.fori_loop(0, heads, sent, 0)
 
-    def sent_block(index, _):
-        da, rest = index // (nb * nc), lax.rem(index, nb * nc)
-        db, dc = rest // nc, lax.rem(rest, nc)
-        arrival(da, db, dc).wait_send()
-        for ds in range(1, peers):
-            mirror(da, db, dc, ds, s).wait_send()
+    def sent_plane(plane, _):
+        for db in range(nb):
+            for dc in range(nc):
+                if db or dc:
+                    arrival(plane, db, dc).wait_send()
+
+                def wait():
+                    for ds in range(1, peers):
+                        mirror(plane, db, dc, ds, s).wait_send()
+
+                if db or dc:
+                    wait()
+                else:
+                    pl.when(plane != a)(wait)
+
+        @pl.when(jnp.logical_and(plane <= a, a < Z - 1))
+        def _():
+            climb(plane, 1).wait_send()
+
+        @pl.when(jnp.logical_and(plane >= a, a > 0))
+        def _():
+            climb(plane, 0).wait_send()
+
         return 0
 
-    lax.fori_loop(1, Z * nb * nc, sent_block, 0)
-    for store in stores:
-        store.wait()
+    lax.fori_loop(0, Z, sent_plane, 0)
 
 
 def local(grid, peers, queries, keys, values, gate_rate, segment_ids, decay_exps, out_weight):
@@ -358,10 +432,10 @@
     anywhere = pl.BlockSpec(memory_space=pl.ANY)
     call = pl.pallas_call(
         functools.partial(kernel, grid, peers, heads, chunk),
-        out_shape=jax.ShapeDtypeStruct((length, columns), bf16),
+        out_shape=pltpu.VMEM((length, columns), bf16),
         in_specs=[anywhere] * 4
         + [pl.BlockSpec(memory_space=pltpu.VMEM), pl.BlockSpec(memory_space=pltpu.SMEM), anywhere],
-        out_specs=anywhere,
+        out_specs=pl.BlockSpec(memory_space=pltpu.VMEM),
         scratch_shapes=[
             pltpu.VMEM((length, key_features), bf16),
             pltpu.VMEM((length, key_features), bf16),
@@ -370,22 +444,21 @@
             pltpu.VMEM((features, columns), bf16),
             pltpu.VMEM((length, features), bf16),
             pltpu.VMEM((length, columns), f32),
-            pltpu.VMEM((length, columns), bf16),
             pltpu.VMEM((1, length), jnp.int32),
             pltpu.VMEM((heads, vw, kw), f32),
             pltpu.VMEM((heads, vw, kw), f32),
             pltpu.SemaphoreType.DMA((5,)),
-            pltpu.SemaphoreType.DMA((columns // TILE,)),
             pltpu.SemaphoreType.DMA((2,)),
             pltpu.SemaphoreType.DMA((heads,)),
             pltpu.SemaphoreType.DMA((heads,)),
             pltpu.SemaphoreType.DMA((chips,)),
             pltpu.SemaphoreType.DMA((chips,)),
+            pltpu.SemaphoreType.DMA((2, grid[0])),
             pltpu.SemaphoreType.DMA((max(peers - 1, 1), chips)),
             pltpu.SemaphoreType.DMA((max(peers - 1, 1), chips)),
         ],
         compiler_params=pltpu.CompilerParams(
-            collective_id=0, has_side_effects=True, vmem_limit_bytes=60 * 1024 * 1024
+            collective_id=0, has_side_effects=True, vmem_limit_bytes=61 * 1024 * 1024
         ),
         name="gla_project",
     )

time: 58.8 us -> 48.2 us (0.82)
  the two profiles are of different devices: /device:TPU:17 before, /device:TPU:0 now
where the time goes in v2:
time: 48.2 us; the launch traced here: 48 us
  Pallas kernels  46.7 us (97%)
  local copies, waits for them, and re-layouts  1.32 us (3%)
    pallas_call x1, Pallas kernels, local(): call(queries[n], keys[n], values[n], gate_rate[n], segment_ids[n:n + 1],...  46.7 us
    unnamed x1, local copies, waits for them, and re-layouts  1.32 us

profile of v2, /device:TPU:0, one launch (start us, length us, event | category | flops | bytes accessed | tf_op | source)
XLA Modules:
  0.0 48.0 jit_solution(1965594679093055702)
XLA Ops:
  0.0 46.7 %gla_project.1 = bf16[512,2048]{1,0:T(8,128)(2,1)S(1)} custom-call(bf16[512,1024]{1,0:T(8,128)(2,1)} %bitcast.7, bf16[512,1024]{1,0:T(8,128)(2,1)} %bitcast.8, bf16[512,2048]{1,0:T(8,128)(2,1)} %bitcast.6, bf16[512,1024]{1,0:T(8,128)(2,1)} %bitcast.9, s32[1,512]{1,0:T(1,128)} %seg_ref.1, s32[4]{0:T(128)} %exps_ref.1, bf16[128,2048]{1,0:T(8,128)(2,1)} %w_hbm.1), custom_call_target="tpu_custom_call" | custom-call | tf_op jit(solution)/shard_map/gla_project/pallas_call | solution.py:466
  46.7 1.3 %copy.9 = bf16[1,512,2048]{2,1,0:T(8,128)(2,1)} copy(bf16[1,512,2048]{2,1,0:T(8,128)(2,1)S(1)} %bitcast.5) | data formatting | bytes 4194304
